TPU v7x, 32 devices: a whole 2x2x4 slice. The times are simulated.
32 devices in a mesh: fsdp: 4 (over y, x), tenant: 4 (over z), dp: 2 (over core).
Axes of the slice: x: 2, y: 2, z: 4, core: 2. Of those that a mesh axis runs over, the one named last changes fastest.
Arguments:
- tokens: bfloat16 [3072, 5120], P(('fsdp', 'dp'), 'tenant'), may hold values from -6 to 6
- block_tenant_index: int32 [48], P(('fsdp', 'dp')), may hold values from 0 to 7
- ranks: int32 [8], replicated, may hold values from 16 to 64, as said below
- frozen_up_weight: bfloat16 [5120, 14336], P(('fsdp', 'dp'), 'tenant'), may hold values from -0.078125 to 0.078125
- tenant_down_adapters: bfloat16 [8, 64, 5120], P('tenant'), may hold values from -0.078125 to 0.078125
- tenant_up_adapters: bfloat16 [8, 64, 14336], P('tenant'), may hold values from -0.75 to 0.75
- cotangent: bfloat16 [3072, 14336], P(('fsdp', 'dp'), 'tenant'), may hold values from -6 to 6
Outputs:
- hidden_out: bfloat16 [3072, 14336], P(('fsdp', 'dp'), 'tenant')
- grad_tokens: bfloat16 [3072, 5120], P(('fsdp', 'dp'), 'tenant')
- grad_down: float32 [8, 64, 5120], P('dp', None, 'tenant')
- grad_up: float32 [8, 64, 14336], P('dp', None, 'tenant')
Inputs may be any that keep to these rules, and one draw needn't show every extreme that they name: `ranks`: multiples of 16; some tenant has rank 64.
All inputs are finite; a program needn't handle non-finite values.
Results may differ from a plain program's by a relative error of at most 0.0034.
Values may be sent and summed in bfloat16 or wider, within the bound.
No kernel may reach another device: no remote copies, remote signals or barrier semaphores. Data moves between devices by JAX's collectives and lax.ppermute only.
A program may use at most 128 MiB of HBM per device.

v0:
```python
import jax
import jax.numpy as jnp
from jax import lax
from jax.sharding import PartitionSpec as P

BLOCK = 64
alpha_scale = 32.0


def make_gain(block_tenant_index, ranks, rows, largest_rank):
    tenants = ranks.shape[0]
    rows_tenant = jnp.repeat(block_tenant_index, BLOCK, total_repeat_length=rows)
    columns = jnp.arange(tenants * largest_rank, dtype=jnp.int32)
    col_tenant = columns // largest_rank
    col_slot = columns % largest_rank
    ranks_col = jnp.repeat(ranks, largest_rank, total_repeat_length=tenants * largest_rank)
    keep = (rows_tenant[:, None] == col_tenant[None, :]) & (col_slot[None, :] < ranks_col[None, :])
    scale_col = alpha_scale / ranks_col.astype(jnp.float32)
    return jnp.where(keep, scale_col[None, :], jnp.float32(0.0))


def shards(
    tokens,
    block_tenant_index,
    ranks,
    frozen_up_weight,
    tenant_down_adapters,
    tenant_up_adapters,
    cotangent,
):
    rows = tokens.shape[0]
    local_d = tokens.shape[1]
    local_f = cotangent.shape[1]
    tenants = ranks.shape[0]
    largest_rank = tenant_down_adapters.shape[1]
    gain = make_gain(block_tenant_index, ranks, rows, largest_rank)
    whole = lax.all_gather(tokens, "tenant", axis=1, tiled=True)
    weight = lax.all_gather(frozen_up_weight, ("fsdp", "dp"), axis=0, tiled=True)
    down_part, up_adapter_slice = (
        lax.all_to_all(tenant_down_adapters, "tenant", split_axis=2, concat_axis=0, tiled=True),
        lax.all_to_all(tenant_up_adapters, "tenant", split_axis=2, concat_axis=0, tiled=True),
    )
    local_down = down_part.reshape(tenants * largest_rank, local_d)
    partial_proj = lax.dot_general(
        tokens, local_down, (((1,), (1,)), ((), ())), preferred_element_type=jnp.float32
    )
    proj = lax.psum(partial_proj, "tenant")
    flattened_up = up_adapter_slice.reshape(tenants * largest_rank, local_f)
    adapted = (proj * gain).astype(jnp.bfloat16)
    base = jnp.dot(whole, weight, preferred_element_type=jnp.float32)
    hidden_out = (base + jnp.dot(adapted, flattened_up, preferred_element_type=jnp.float32)).astype(
        jnp.bfloat16
    )
    back_part = lax.dot_general(
        cotangent, flattened_up, (((1,), (1,)), ((), ())), preferred_element_type=jnp.float32
    )
    back = lax.psum(back_part, "tenant")
    adapted_grad = (back * gain).astype(jnp.bfloat16)
    base_back = lax.dot_general(
        cotangent, weight, (((1,), (1,)), ((), ())), preferred_element_type=jnp.float32
    )
    grad_base = lax.psum_scatter(base_back, "tenant", scatter_dimension=1, tiled=True)
    grad_tokens = (
        grad_base + jnp.dot(adapted_grad, local_down, preferred_element_type=jnp.float32)
    ).astype(jnp.bfloat16)
    up_term = lax.dot_general(
        adapted, cotangent, (((0,), (0,)), ((), ())), preferred_element_type=jnp.float32
    )
    down_term = lax.dot_general(
        adapted_grad, tokens, (((0,), (0,)), ((), ())), preferred_element_type=jnp.float32
    )
    up_term = up_term.reshape(tenants, largest_rank, local_f)
    down_term = down_term.reshape(tenants, largest_rank, local_d)
    down_share, up_share = (
        lax.psum_scatter(down_term, "dp", scatter_dimension=0, tiled=True),
        lax.psum_scatter(up_term, "dp", scatter_dimension=0, tiled=True),
    )
    grad_down, grad_up = lax.psum((down_share, up_share), "fsdp")
    return (hidden_out, grad_tokens, grad_down, grad_up)


def solution(mesh):
    return jax.shard_map(
        shards,
        mesh=mesh,
        in_specs=(
            P(("fsdp", "dp"), "tenant"),
            P(("fsdp", "dp")),
            P(),
            P(("fsdp", "dp"), "tenant"),
            P("tenant", None, None),
            P("tenant", None, None),
            P(("fsdp", "dp"), "tenant"),
        ),
        out_specs=(
            P(("fsdp", "dp"), "tenant"),
            P(("fsdp", "dp"), "tenant"),
            P("dp", None, "tenant"),
            P("dp", None, "tenant"),
        ),
        check_vma=False,
    )
```

profile of v0, /device:TPU:0, one launch (start us, length us, event | category | flops | bytes accessed | tf_op | source)
XLA Modules:
  0.0 692.7 jit_solution(15375952981959615952)
XLA Ops:
  8.0 6.4 copy.13
  14.5 4.7 reshape.322
  19.1 6.3 all-to-all-start
  25.5 15.8 %copy.16 = bf16[2,64,14336]{1,0,2:T(2,128)(2,1)} copy(bf16[2,64,14336]{2,1,0:T(8,128)(2,1)} %param.16) | data formatting | bytes 7340032 | tf_op args[5]
  41.3 8.6 %reshape.320 = bf16[4,2,229376]{2,1,0:T(2,128)(2,1)} reshape(bf16[14336,2,64]{2,1,0:T(2,128)(2,1)} %bitcast.77) | data formatting | bytes 7340032
  49.9 7.1 %all-to-all-done = bf16[4,2,81920]{2,1,0:T(2,128)(2,1)} async-done(((bf16[4,2,81920]{2,1,0:T(2,128)(2,1)}), bf16[4,2,81920]{2,1,0:T(2,128)(2,1)}, u32[]{:S(2)}, u32[]{:S(2)}) %all-to-all-start) | async-done | bytes 1310752 | tf_op jit(solution)/shard_map/all_to_all | solution.py:40
  56.9 4.8 all-to-all-start.1
  61.8 0.0 all-reduce.5.cloned.1.call-start
  61.8 4.6 reshape.323
  66.4 7.4 %copy.19 = bf16[2,64,4,1280]{3,2,1,0:T(4,128)(2,1)} copy(bf16[2,64,4,1280]{1,0,3,2:T(2,128)(2,1)} %bitcast.82) | data formatting | bytes 2621440 | tf_op jit(solution)/shard_map/all_to_all | solution.py:40
  73.8 1.4 copy.15
  75.3 1.0 copy-done.3
  76.3 2.8 fusion.26
  79.1 64.2 %all-to-all-done.1 = bf16[4,2,229376]{2,1,0:T(2,128)(2,1)} async-done(((bf16[4,2,229376]{2,1,0:T(2,128)(2,1)}), bf16[4,2,229376]{2,1,0:T(2,128)(2,1)}, u32[]{:S(2)}, u32[]{:S(2)}) %all-to-all-start.1) | async-done | bytes 3670048 | tf_op jit(solution)/shard_map/all_to_all | solution.py:41
  143.3 8.4 %reshape.321 = bf16[14336,2,64]{2,1,0:T(2,128)(2,1)} reshape(bf16[4,2,229376]{2,1,0:T(2,128)(2,1)} %all-to-all-done.1) | data formatting | bytes 7340032
  151.7 18.7 %copy.20 = bf16[2,64,4,3584]{3,2,1,0:T(4,128)(2,1)} copy(bf16[2,64,4,3584]{1,0,3,2:T(2,128)(2,1)} %bitcast.76) | data formatting | bytes 7340032 | tf_op jit(solution)/shard_map/all_to_all | solution.py:41
  170.4 2.7 copy.18
  173.1 1.8 copy-done.2
  174.9 2.5 fusion.28
  177.5 0.0 all-gather.5.cloned.1.call-start
  177.5 0.5 all-gather.5.cloned.1.call-update
  178.0 0.0 reduce-scatter.6.cloned.1.call-start
  178.1 0.7 fusion.23
  178.8 0.7 fusion.24
  179.5 0.1 add_add_fusion.1
  179.6 0.1 fusion.8
  179.7 3.8 fusion.16
  183.5 4.5 compare_select_fusion.2
  188.0 0.8 fusion.12
  188.8 0.1 and_select_fusion
  188.9 56.8 %all-reduce.5.cloned.1.call-done = (f32[384,512]{1,0:T(8,128)}, f32[384,512]{1,0:T(8,128)}) async-done(((f32[384,512]{1,0:T(8,128)}, f32[384,512]{1,0:T(8,128)}), (f32[384,512]{1,0:T(8,128)}, f32[384,512]{1,0:T(8,128)})) %all-reduce.5.cloned.1.call-update) | async-done | bytes 1572880 | tf_op jit(solution)/shard_map/psum | solution.py:47
  245.7 4.0 fusion.17
  249.8 7.1 %fusion.20 = f32[512,3584]{1,0:T(8,128)} fusion(bf16[384,3584]{1,0:T(8,128)(2,1)S(1)} %copy-done, f32[384,512]{1,0:T(8,128)S(1)} %copy-done.5, f32[512]{0:T(512)S(1)} %convert_divide_fusion, s32[512]{0:T(512)S(1)} %add_select_fusion, s32[384]{0:T(512)S(1)} %and_select_fusion, pred[512]{0:T(512)(128)(4,1)S(1)} %get-tuple-element.32), kind=kOutput, calls=%fused_computation.52 | convolution fusion | flops 1410269184 | bytes 10885120 | tf_op jit(solution)/shard_map/dot_general | solution.py:66
  256.9 0.0 all-gather.3.cloned.1.call-start
  256.9 0.5 all-gather.3.cloned.1.call-update
  257.5 0.2 reduce-scatter.4.cloned.1.call-start
  257.7 96.2 %all-gather.5.cloned.1.call-done = bf16[5120,3584]{1,0:T(8,128)(2,1)} async-done(((bf16[640,3584]{1,0:T(8,128)(2,1)}), bf16[5120,3584]{1,0:T(8,128)(2,1)}) %all-gather.5.cloned.1.call-update) | async-done | bytes 36700176 | tf_op jit(solution)/shard_map/all_gather | solution.py:38
  353.9 22.1 %fusion.27 = f32[384,5120]{1,0:T(8,128)} fusion(bf16[384,3584]{1,0:T(8,128)(2,1)S(1)} %copy-done, bf16[5120,3584]{1,0:T(8,128)(2,1)} %all-gather.5.cloned.1.call-done), kind=kOutput, calls=%fused_computation.57 | convolution fusion | flops 14092861440 | bytes 47316992 | tf_op jit(solution)/shard_map/dot_general | solution.py:59
  376.0 0.0 all-reduce.7.cloned.1.call-start
  376.1 0.5 all-reduce.7.cloned.1.call-update
  376.6 139.9 %all-gather.3.cloned.1.call-done = bf16[384,5120]{1,0:T(8,128)(2,1)} async-done(((bf16[384,1280]{1,0:T(8,128)(2,1)}), bf16[384,5120]{1,0:T(8,128)(2,1)}) %all-gather.3.cloned.1.call-update) | async-done | bytes 3932176 | tf_op jit(solution)/shard_map/all_gather | solution.py:37
  516.5 23.5 %fusion.25 = f32[384,3584]{1,0:T(8,128)} fusion(bf16[384,5120]{1,0:T(8,128)(2,1)} %all-gather.3.cloned.1.call-done, bf16[5120,3584]{1,0:T(8,128)(2,1)} %all-gather.5.cloned.1.call-done), kind=kOutput, calls=%fused_computation.55 | convolution fusion | flops 14092861440 | bytes 46137344 | tf_op jit(solution)/shard_map/dot_general | solution.py:50
  540.0 7.0 %fusion = bf16[384,3584]{1,0:T(8,128)(2,1)} fusion(f32[384,3584]{1,0:T(8,128)} %fusion.25, bf16[512,3584]{1,0:T(8,128)(2,1)} %bitcast.79, f32[384,512]{1,0:T(8,128)S(1)} %copy-done.5, f32[512]{0:T(512)S(1)} %convert_divide_fusion, s32[512]{0:T(512)S(1)} %add_select_fusion, s32[384]{0:T(512)S(1)} %and_select_fusion, pred[512]{0:T(512)(128)(4,1)S(1)} %get-tuple-element.32), kind=kOutput, calls=%fused_computation.1 | convolution fusion | flops 1413021696 | bytes 12720128 | tf_op jit(solution)/shard_map/dot_general | solution.py:51
  547.0 10.7 %reduce-scatter.4.cloned.1.call-done = f32[384,1280]{1,0:T(8,128)} async-done(((f32[384,5120]{1,0:T(8,128)}), f32[384,1280]{1,0:T(8,128)}) %reduce-scatter.4.cloned.1.call-update) | async-done | bytes 1966096 | tf_op jit(solution)/shard_map/reduce_scatter | solution.py:62
  557.7 3.3 fusion.1
  561.0 117.8 %all-reduce.7.cloned.1.call-done = (f32[4,64,1280]{2,1,0:T(8,128)}, f32[4,64,3584]{2,1,0:T(8,128)}) async-done(((f32[4,64,1280]{2,1,0:T(8,128)}, f32[4,64,3584]{2,1,0:T(8,128)}), (f32[4,64,1280]{2,1,0:T(8,128)}, f32[4,64,3584]{2,1,0:T(8,128)})) %all-reduce.7.cloned.1.call-update) | async-done | bytes 4980752 | tf_op jit(solution)/shard_map/psum | solution.py:78
  678.8 2.6 copy.29
  681.4 4.1 copy.30
  (32 shorter events, 0.2 us)
Async XLA Ops:
  8.0 166.9 %copy-start = (bf16[384,3584]{1,0:T(8,128)(2,1)S(1)}, bf16[384,3584]{1,0:T(8,128)(2,1)}, u32[]{:S(2)}) copy-start(bf16[384,3584]{1,0:T(8,128)(2,1)} %param.17) | copy-start | bytes 8257540
  19.1 37.8 %all-to-all-start = ((bf16[4,2,81920]{2,1,0:T(2,128)(2,1)}), bf16[4,2,81920]{2,1,0:T(2,128)(2,1)}, u32[]{:S(2)}, u32[]{:S(2)}) async-start(bf16[4,2,81920]{2,1,0:T(2,128)(2,1)} %reshape.322), calls=%async_computation | async-start | bytes 2621440 | tf_op jit(solution)/shard_map/all_to_all | solution.py:40
  56.9 86.3 %all-to-all-start.1 = ((bf16[4,2,229376]{2,1,0:T(2,128)(2,1)}), bf16[4,2,229376]{2,1,0:T(2,128)(2,1)}, u32[]{:S(2)}, u32[]{:S(2)}) async-start(bf16[4,2,229376]{2,1,0:T(2,128)(2,1)} %reshape.320), calls=%async_computation.1 | async-start | bytes 7340032 | tf_op jit(solution)/shard_map/all_to_all | solution.py:41
  61.8 184.0 %all-reduce.5.cloned.1.call-start = ((), (), s32[]{:S(2)}) async-start(), calls=%async_computation.10 | async-start | bytes 3145728 | tf_op jit(solution)/shard_map/psum | solution.py:47
  75.3 1.1 copy-start.3
  173.1 1.8 copy-start.2
  177.4 0.7 copy-start.8
  177.4 1.4 copy-start.7
  177.4 2.1 copy-start.10
  177.4 2.2 copy-start.9
  177.5 176.5 %all-gather.5.cloned.1.call-start = ((), (), s32[]{:S(2)}) async-start(), calls=%async_computation.6 | async-start | bytes 41287680 | tf_op jit(solution)/shard_map/all_gather | solution.py:38
  178.0 198.0 %reduce-scatter.6.cloned.1.call-start = ((), (), s32[]{:S(2)}) async-start(), calls=%async_computation.8 | async-start | bytes 3932160 | tf_op jit(solution)/shard_map/reduce_scatter | solution.py:75
  245.7 4.1 copy-start.5
  249.7 126.4 %reduce-scatter.8.cloned.1.call-start = ((), (), s32[]{:S(2)}) async-start(), calls=%async_computation.9 | async-start | bytes 11010048 | tf_op jit(solution)/shard_map/reduce_scatter | solution.py:76
  256.9 259.6 %all-gather.3.cloned.1.call-start = ((), (), s32[]{:S(2)}) async-start(), calls=%async_computation.5 | async-start | bytes 4915200 | tf_op jit(solution)/shard_map/all_gather | solution.py:37
  257.5 300.2 %reduce-scatter.4.cloned.1.call-start = ((), (), s32[]{:S(2)}) async-start(), calls=%async_computation.7 | async-start | bytes 9830400 | tf_op jit(solution)/shard_map/reduce_scatter | solution.py:62
  376.0 302.8 %all-reduce.7.cloned.1.call-start = ((), (), s32[]{:S(2)}) async-start(), calls=%async_computation.11 | async-start | bytes 9961472 | tf_op jit(solution)/shard_map/psum | solution.py:78
  540.0 17.8 %copy-start.4 = (bf16[4,2,64,1280]{3,2,1,0:T(8,128)(2,1)S(1)}, bf16[4,2,64,1280]{3,2,1,0:T(8,128)(2,1)}, u32[]{:S(2)}) copy-start(bf16[4,2,64,1280]{3,2,1,0:T(8,128)(2,1)} %copy-done.3) | copy-start | bytes 3932164
  540.0 17.8 %copy-start.6 = (f32[384,512]{1,0:T(8,128)S(1)}, f32[384,512]{1,0:T(8,128)}, u32[]{:S(2)}) copy-start(f32[384,512]{1,0:T(8,128)} %get-tuple-element.29) | copy-start | bytes 2359300
  678.8 6.8 copy-start.1
Sparse Core Ops, SparseCore 0:
  177.6 68.0 all-reduce.4
  249.9 16.8 reduce-scatter.5
  269.1 17.2 reduce-scatter.7
  376.1 181.5 reduce-scatter.3
  561.2 117.5 all-reduce.6
Sparse Core Ops, SparseCore 1:
  179.9 174.0 all-gather.4
  355.4 161.1 all-gather.2
where the time goes:
time: 695 us; the launch traced here: 693 us
  waiting for transfers between devices  494 us (71%)
  local copies, waits for them, and re-layouts  89.8 us (13%)
  matrix products  72.2 us (10%)
  between operations  15.4 us (2%)
  starting transfers between devices  11.6 us (2%)
  other arithmetic  9.35 us (1%)
    all_gather x1, waiting for transfers between devices, shards(): whole = lax.all_gather(tokens, 'tenant', axis=1, tiled=True)  140 us
    psum x1, waiting for transfers between devices, shards(): grad_down, grad_up = lax.psum((down_share, up_share), 'fsdp')  118 us
    all_gather x1, waiting for transfers between devices, shards(): lax.all_gather(frozen_up_weight, ('fsdp', 'dp'), axis=0, tiled=True)  96.2 us
    all_to_all x1, waiting for transfers between devices, shards(): lax.all_to_all(tenant_up_adapters, 'tenant', split_axis=2, concat_axis=0,...  64.2 us
    unnamed x30, local copies, waits for them, and re-layouts  58.2 us
    psum x1, waiting for transfers between devices, shards(): proj = lax.psum(partial_proj, 'tenant')  56.8 us
    dot_general x1, matrix products, shards(): base = jnp.dot(whole, weight, preferred_element_type=jnp.float32)  23.5 us
    dot_general x1, matrix products, shards(): lax.dot_general(cotangent, weight, (((1,), (1,)), ((), ())), preferred_el...  22.1 us
  transfers between devices with their start and end apart: 9, of which 7 were waited for; matrix products, arithmetic and copies ran while one was open for 17% of the time, Pallas kernels for 0%

commit v1 on v0

--- a/solution.py
+++ b/solution.py
@@ -38,7 +38,15 @@
     weight = lax.all_gather(frozen_up_weight, ("fsdp", "dp"), axis=0, tiled=True)
     down_part, up_adapter_slice = (
         lax.all_to_all(tenant_down_adapters, "tenant", split_axis=2, concat_axis=0, tiled=True),
-        lax.all_to_all(tenant_up_adapters, "tenant", split_axis=2, concat_axis=0, tiled=True),
+        jnp.concatenate(
+            lax.all_to_all(
+                jnp.stack(jnp.split(tenant_up_adapters, lax.axis_size("tenant"), axis=2)),
+                "tenant",
+                0,
+                0,
+            ),
+            axis=0,
+        ),
     )
     local_down = down_part.reshape(tenants * largest_rank, local_d)
     partial_proj = lax.dot_general(

time: 695 us -> 664 us (0.955)
  local copies, waits for them, and re-layouts: 89.8 us -> 36.2 us
  waiting for transfers between devices: 494 us -> 514 us
    unnamed x30 -> x25, local copies, waits for them, and re-layouts: 58.2 us -> 23.6 us
    all_to_all x2 -> x0, local copies, waits for them, and re-layouts: 21.4 us -> none  [shards(): lax.all_to_all(tenant_up_adapters, 'tenant', split_axis=2, concat_axis=0,...]
    all_to_all x1, waiting for transfers between devices: 7.06 us -> 27 us  [shards(): lax.all_to_all(tenant_down_adapters, 'tenant', split_axis=2, concat_axis=...]
  transfers between devices with their start and end apart: 9 -> 9, of which waited for: 7 -> 7; matrix products, arithmetic and copies ran while one was open for 17% -> 15% of each run, Pallas kernels for 0% -> 0%
where the time goes in v1:
time: 664 us; the launch traced here: 663 us
  waiting for transfers between devices  514 us (77%)
  matrix products  74.2 us (11%)
  local copies, waits for them, and re-layouts  36.2 us (5%)
  between operations  15.4 us (2%)
  starting transfers between devices  11.6 us (2%)
  other arithmetic  11.3 us (2%)
    all_gather x1, waiting for transfers between devices, shards(): whole = lax.all_gather(tokens, 'tenant', axis=1, tiled=True)  140 us
    psum x1, waiting for transfers between devices, shards(): grad_down, grad_up = lax.psum((down_share, up_share), 'fsdp')  118 us
    all_gather x1, waiting for transfers between devices, shards(): lax.all_gather(frozen_up_weight, ('fsdp', 'dp'), axis=0, tiled=True)  96.4 us
    all_to_all x1, waiting for transfers between devices, shards(): lax.all_to_all(jnp.stack(jnp.split(tenant_up_adapters, lax.axis_size('ten...  64.2 us
    psum x1, waiting for transfers between devices, shards(): proj = lax.psum(partial_proj, 'tenant')  57 us
    all_to_all x1, waiting for transfers between devices, shards(): lax.all_to_all(tenant_down_adapters, 'tenant', split_axis=2, concat_axis=...  27 us
    unnamed x25, local copies, waits for them, and re-layouts  23.6 us
    dot_general x1, matrix products, shards(): base = jnp.dot(whole, weight, preferred_element_type=jnp.float32)  23.5 us
  transfers between devices with their start and end apart: 9, of which 7 were waited for; matrix products, arithmetic and copies ran while one was open for 15% of the time, Pallas kernels for 0%

profile of v1, /device:TPU:0, one launch (start us, length us, event | category | flops | bytes accessed | tf_op | source)
XLA Modules:
  0.0 663.0 jit_solution(16354701321059353911)
XLA Ops:
  8.0 6.4 copy.15
  14.5 4.7 reshape.315
  19.1 6.3 all-to-all-start
  25.5 2.4 slice_bitcast_fusion.3
  27.9 2.1 pad_maximum_fusion
  29.9 27.0 %all-to-all-done = bf16[4,2,81920]{2,1,0:T(2,128)(2,1)} async-done(((bf16[4,2,81920]{2,1,0:T(2,128)(2,1)}), bf16[4,2,81920]{2,1,0:T(2,128)(2,1)}, u32[]{:S(2)}, u32[]{:S(2)}) %all-to-all-start) | async-done | bytes 1310752 | tf_op jit(solution)/shard_map/all_to_all | solution.py:40
  56.9 4.8 all-to-all-start.1
  61.7 0.0 all-reduce.5.cloned.1.call-start
  61.8 4.6 reshape.316
  66.4 7.4 %copy.20 = bf16[2,64,4,1280]{3,2,1,0:T(4,128)(2,1)} copy(bf16[2,64,4,1280]{1,0,3,2:T(2,128)(2,1)} %bitcast.83) | data formatting | bytes 2621440 | tf_op jit(solution)/shard_map/all_to_all | solution.py:40
  73.8 1.4 copy.17
  75.2 1.0 copy-done.2
  76.3 2.8 fusion.26
  79.1 64.2 %all-to-all-done.1 = bf16[4,2,64,3584]{3,2,1,0:T(8,128)(2,1)} async-done(((bf16[4,2,64,3584]{3,2,1,0:T(8,128)(2,1)}), bf16[4,2,64,3584]{3,2,1,0:T(8,128)(2,1)}, u32[]{:S(2)}, u32[]{:S(2)}) %all-to-all-start.1) | async-done | bytes 3670048 | tf_op jit(solution)/shard_map/all_to_all | solution.py:42
  143.2 4.5 convolution_bitcast_fusion
  147.8 0.0 all-reduce.5.cloned.1.call-update
  147.8 0.0 all-gather.5.cloned.1.call-start
  147.9 0.5 all-gather.5.cloned.1.call-update
  148.4 0.0 reduce-scatter.6.cloned.1.call-start
  148.5 0.7 fusion.23
  149.1 0.7 fusion.24
  149.8 0.1 add_add_fusion.1
  149.9 0.1 fusion.8
  150.0 3.9 fusion.16
  153.9 4.3 compare_select_fusion.2
  158.2 0.7 fusion.12
  158.9 0.1 and_select_fusion
  159.0 57.0 %all-reduce.5.cloned.1.call-done = (f32[384,512]{1,0:T(8,128)}, f32[384,512]{1,0:T(8,128)}) async-done(((f32[384,512]{1,0:T(8,128)}, f32[384,512]{1,0:T(8,128)}), (f32[384,512]{1,0:T(8,128)}, f32[384,512]{1,0:T(8,128)})) %all-reduce.5.cloned.1.call-update) | async-done | bytes 1572880 | tf_op jit(solution)/shard_map/psum | solution.py:55
  216.0 4.0 fusion.17
  220.1 0.0 reduce-scatter.8.cloned.1.call-start
  220.1 7.1 %fusion.20 = f32[512,3584]{1,0:T(8,128)} fusion(bf16[384,3584]{1,0:T(8,128)(2,1)S(1)} %copy-done, f32[384,512]{1,0:T(8,128)S(1)} %copy-done.4, f32[512]{0:T(512)S(1)} %convert_divide_fusion, s32[512]{0:T(512)S(1)} %add_select_fusion, s32[384]{0:T(512)S(1)} %and_select_fusion, pred[512]{0:T(512)(128)(4,1)S(1)} %get-tuple-element.32), kind=kOutput, calls=%fused_computation.58 | convolution fusion | flops 1410269184 | bytes 10885120 | tf_op jit(solution)/shard_map/dot_general | solution.py:74
  227.2 0.0 all-gather.3.cloned.1.call-start
  227.3 0.5 all-gather.3.cloned.1.call-update
  227.8 0.0 reduce-scatter.4.cloned.1.call-start
  227.9 96.4 %all-gather.5.cloned.1.call-done = bf16[5120,3584]{1,0:T(8,128)(2,1)} async-done(((bf16[640,3584]{1,0:T(8,128)(2,1)}), bf16[5120,3584]{1,0:T(8,128)(2,1)}) %all-gather.5.cloned.1.call-update) | async-done | bytes 36700176 | tf_op jit(solution)/shard_map/all_gather | solution.py:38
  324.3 22.1 %fusion.27 = f32[384,5120]{1,0:T(8,128)} fusion(bf16[384,3584]{1,0:T(8,128)(2,1)S(1)} %copy-done, bf16[5120,3584]{1,0:T(8,128)(2,1)} %all-gather.5.cloned.1.call-done), kind=kOutput, calls=%fused_computation.63 | convolution fusion | flops 14092861440 | bytes 47316992 | tf_op jit(solution)/shard_map/dot_general | solution.py:67
  346.4 0.2 all-reduce.7.cloned.1.call-start
  346.6 0.0 reduce-scatter.6.cloned.1.call-done
  346.6 0.0 reduce-scatter.8.cloned.1.call-done
  346.7 0.3 all-reduce.7.cloned.1.call-update
  347.0 139.9 %all-gather.3.cloned.1.call-done = bf16[384,5120]{1,0:T(8,128)(2,1)} async-done(((bf16[384,1280]{1,0:T(8,128)(2,1)}), bf16[384,5120]{1,0:T(8,128)(2,1)}) %all-gather.3.cloned.1.call-update) | async-done | bytes 3932176 | tf_op jit(solution)/shard_map/all_gather | solution.py:37
  486.8 23.5 %fusion.25 = f32[384,3584]{1,0:T(8,128)} fusion(bf16[384,5120]{1,0:T(8,128)(2,1)} %all-gather.3.cloned.1.call-done, bf16[5120,3584]{1,0:T(8,128)(2,1)} %all-gather.5.cloned.1.call-done), kind=kOutput, calls=%fused_computation.61 | convolution fusion | flops 14092861440 | bytes 46137344 | tf_op jit(solution)/shard_map/dot_general | solution.py:58
  510.3 7.0 %fusion = bf16[384,3584]{1,0:T(8,128)(2,1)} fusion(f32[384,3584]{1,0:T(8,128)} %fusion.25, bf16[512,3584]{1,0:T(8,128)(2,1)} %bitcast.28, f32[384,512]{1,0:T(8,128)S(1)} %copy-done.4, f32[512]{0:T(512)S(1)} %convert_divide_fusion, s32[512]{0:T(512)S(1)} %add_select_fusion, s32[384]{0:T(512)S(1)} %and_select_fusion, pred[512]{0:T(512)(128)(4,1)S(1)} %get-tuple-element.32), kind=kOutput, calls=%fused_computation.1 | convolution fusion | flops 1413021696 | bytes 12720128 | tf_op jit(solution)/shard_map/dot_general | solution.py:59
  517.3 10.7 %reduce-scatter.4.cloned.1.call-done = f32[384,1280]{1,0:T(8,128)} async-done(((f32[384,5120]{1,0:T(8,128)}), f32[384,1280]{1,0:T(8,128)}) %reduce-scatter.4.cloned.1.call-update) | async-done | bytes 1966096 | tf_op jit(solution)/shard_map/reduce_scatter | solution.py:70
  528.1 3.3 fusion.1
  531.4 117.8 %all-reduce.7.cloned.1.call-done = (f32[4,64,1280]{2,1,0:T(8,128)}, f32[4,64,3584]{2,1,0:T(8,128)}) async-done(((f32[4,64,1280]{2,1,0:T(8,128)}, f32[4,64,3584]{2,1,0:T(8,128)}), (f32[4,64,1280]{2,1,0:T(8,128)}, f32[4,64,3584]{2,1,0:T(8,128)})) %all-reduce.7.cloned.1.call-update) | async-done | bytes 4980752 | tf_op jit(solution)/shard_map/psum | solution.py:86
  649.1 2.6 copy.29
  651.8 4.1 copy.30
  (27 shorter events, 0.1 us)
Async XLA Ops:
  8.0 135.2 %copy-start = (bf16[384,3584]{1,0:T(8,128)(2,1)S(1)}, bf16[384,3584]{1,0:T(8,128)(2,1)}, u32[]{:S(2)}) copy-start(bf16[384,3584]{1,0:T(8,128)(2,1)} %param.17) | copy-start | bytes 8257540
  19.1 37.8 %all-to-all-start = ((bf16[4,2,81920]{2,1,0:T(2,128)(2,1)}), bf16[4,2,81920]{2,1,0:T(2,128)(2,1)}, u32[]{:S(2)}, u32[]{:S(2)}) async-start(bf16[4,2,81920]{2,1,0:T(2,128)(2,1)} %reshape.315), calls=%async_computation | async-start | bytes 2621440 | tf_op jit(solution)/shard_map/all_to_all | solution.py:40
  56.9 86.3 %all-to-all-start.1 = ((bf16[4,2,64,3584]{3,2,1,0:T(8,128)(2,1)}), bf16[4,2,64,3584]{3,2,1,0:T(8,128)(2,1)}, u32[]{:S(2)}, u32[]{:S(2)}) async-start(bf16[4,2,64,3584]{3,2,1,0:T(8,128)(2,1)} %pad_maximum_fusion), calls=%async_computation.1 | async-start | bytes 7340032 | tf_op jit(solution)/shard_map/all_to_all | solution.py:42
  61.7 154.3 %all-reduce.5.cloned.1.call-start = ((), (), s32[]{:S(2)}) async-start(), calls=%async_computation.10 | async-start | bytes 3145728 | tf_op jit(solution)/shard_map/psum | solution.py:55
  75.2 1.1 copy-start.2
  147.8 0.7 copy-start.7
  147.8 1.4 copy-start.6
  147.8 2.1 copy-start.9
  147.8 2.2 copy-start.8
  147.8 176.5 %all-gather.5.cloned.1.call-start = ((), (), s32[]{:S(2)}) async-start(), calls=%async_computation.6 | async-start | bytes 41287680 | tf_op jit(solution)/shard_map/all_gather | solution.py:38
  148.4 198.2 %reduce-scatter.6.cloned.1.call-start = ((), (), s32[]{:S(2)}) async-start(), calls=%async_computation.8 | async-start | bytes 3932160 | tf_op jit(solution)/shard_map/reduce_scatter | solution.py:83
  216.0 4.1 copy-start.4
  220.1 126.6 %reduce-scatter.8.cloned.1.call-start = ((), (), s32[]{:S(2)}) async-start(), calls=%async_computation.9 | async-start | bytes 11010048 | tf_op jit(solution)/shard_map/reduce_scatter | solution.py:84
  227.2 259.6 %all-gather.3.cloned.1.call-start = ((), (), s32[]{:S(2)}) async-start(), calls=%async_computation.5 | async-start | bytes 4915200 | tf_op jit(solution)/shard_map/all_gather | solution.py:37
  227.8 300.3 %reduce-scatter.4.cloned.1.call-start = ((), (), s32[]{:S(2)}) async-start(), calls=%async_computation.7 | async-start | bytes 9830400 | tf_op jit(solution)/shard_map/reduce_scatter | solution.py:70
  346.4 302.8 %all-reduce.7.cloned.1.call-start = ((), (), s32[]{:S(2)}) async-start(), calls=%async_computation.11 | async-start | bytes 9961472 | tf_op jit(solution)/shard_map/psum | solution.py:86
  510.3 17.8 %copy-start.3 = (bf16[4,2,64,1280]{3,2,1,0:T(8,128)(2,1)S(1)}, bf16[4,2,64,1280]{3,2,1,0:T(8,128)(2,1)}, u32[]{:S(2)}) copy-start(bf16[4,2,64,1280]{3,2,1,0:T(8,128)(2,1)} %copy-done.2) | copy-start | bytes 3932164
  510.3 17.8 %copy-start.5 = (f32[384,512]{1,0:T(8,128)S(1)}, f32[384,512]{1,0:T(8,128)}, u32[]{:S(2)}) copy-start(f32[384,512]{1,0:T(8,128)} %get-tuple-element.29) | copy-start | bytes 2359300
  649.1 6.8 %copy-start.1 = (bf16[384,3584]{1,0:T(8,128)(2,1)S(1)}, bf16[384,3584]{1,0:T(8,128)(2,1)}, u32[]{:S(2)}) copy-start(bf16[384,3584]{1,0:T(8,128)(2,1)} %param.17) | copy-start | bytes 8257540
Sparse Core Ops, SparseCore 0:
  147.9 68.0 all-reduce.4
  220.2 16.8 reduce-scatter.5
  239.4 17.3 reduce-scatter.7
  346.5 181.5 reduce-scatter.3
  531.5 117.5 all-reduce.6
Sparse Core Ops, SparseCore 1:
  150.2 174.0 all-gather.4
  325.7 161.1 all-gather.2
